TPU v7x, 256 devices: a whole 4x4x8 slice. The times are simulated.
256 devices in a mesh: bank: 16 (over z, core), zero: 16 (over y, x).
Axes of the slice: x: 4, y: 4, z: 8, core: 2. Of those that a mesh axis runs over, the one named last changes fastest.
Arguments:
- master_gate: float32 [64, 2048, 1408], P('bank', 'zero'), may hold values from -0.1875 to 0.1875
- master_up: float32 [64, 2048, 1408], P('bank', 'zero'), may hold values from -0.1875 to 0.1875
- master_down: float32 [64, 1408, 2048], P('bank', None, 'zero'), may hold values from -0.21875 to 0.21875
- router_weight: float32 [2048, 64], P('zero', 'bank'), may hold values from -0.125 to 0.125
- router_gain: float32 [2048], P('zero'), may hold values from 0.25 to 1.75
Outputs:
- final_gate: bfloat16 [64, 2048, 1408], P('bank', None, 'zero')
- final_up: bfloat16 [64, 2048, 1408], P('bank', None, 'zero')
- final_down: bfloat16 [64, 1408, 2048], P('bank', 'zero')
- scale_gate: float32 [64, 1408], P('bank', 'zero')
- scale_up: float32 [64, 1408], P('bank', 'zero')
- scale_down: float32 [64, 1408], P('bank', 'zero')
- serve_router: bfloat16 [2048, 64], replicated
All inputs are finite; a program needn't handle non-finite values. Where the computation divides by a largest or mean magnitude, that divisor is 1e-20 or more.
Results may differ from a plain program's by a relative error of at most 0.0013.
Values may be sent and summed in bfloat16 or wider, within the bound.
A program may use at most 64 MiB of HBM per device.

v0:
```python
import jax
import jax.numpy as jnp
from jax import lax
from jax.sharding import PartitionSpec as P

D_MODEL = 2048


def copy_for_each(x, axis):
    count = lax.axis_size(axis)
    return lax.all_to_all(jnp.broadcast_to(x[None], (count, *x.shape)), axis, 0, 0, tiled=True)


def taken_together(x, axis):
    return copy_for_each(x, axis).sum(axis=0)


def in_one(arrays, axis):
    vector, at, finished = (jnp.concatenate([a.reshape(-1) for a in arrays]), 0, [])
    total = taken_together(vector, axis)
    for a in arrays:
        finished.append(total[at : at + a.size].reshape(a.shape))
        at += a.size
    return tuple(finished)


def side_by_side(arrays, axis, split_dim, concat_dim, along):
    both = jnp.concatenate(arrays, axis=along)
    whole, at, finished = (
        lax.all_to_all(both, axis, split_axis=split_dim, concat_axis=concat_dim, tiled=True),
        0,
        [],
    )
    for a in arrays:
        finished.append(lax.slice_in_dim(whole, at, at + a.shape[along], axis=along))
        at += a.shape[along]
    return tuple(finished)


def laid_out(pieces, dim):
    shape = list(pieces.shape[1:])
    shape[dim] *= pieces.shape[0]
    return jnp.moveaxis(pieces, 0, dim).reshape(shape)


def gather_directly(x, axis, dim):
    pieces = copy_for_each(x, axis)
    return laid_out(pieces, dim)


def local(master_gate, master_up, master_down, router_weight, router_gain):
    total_gate, total_up, total_down = in_one(
        (
            jnp.sum(jnp.abs(master_gate), axis=1),
            jnp.sum(jnp.abs(master_up), axis=1),
            jnp.sum(jnp.abs(master_down), axis=2),
        ),
        "zero",
    )
    scale_gate = total_gate / D_MODEL
    scale_up = total_up / D_MODEL
    scale_down = total_down / D_MODEL
    narrow_gate, narrow_up, narrow_down = (
        (master_gate / jnp.expand_dims(scale_gate, 1)).astype(jnp.bfloat16),
        (master_up / jnp.expand_dims(scale_up, 1)).astype(jnp.bfloat16),
        (master_down / jnp.expand_dims(scale_down, 2)).astype(jnp.bfloat16),
    )
    final_gate, final_up = side_by_side((narrow_gate, narrow_up), "zero", 2, 1, 0)
    final_down = lax.all_to_all(narrow_down, "zero", split_axis=1, concat_axis=2, tiled=True)
    scale_gate = lax.dynamic_slice_in_dim(
        scale_gate, lax.axis_index("zero") * final_gate.shape[2], final_gate.shape[2], axis=1
    )
    scale_up = lax.dynamic_slice_in_dim(
        scale_up, lax.axis_index("zero") * final_up.shape[2], final_up.shape[2], axis=1
    )
    scale_down = lax.dynamic_slice_in_dim(
        scale_down, lax.axis_index("zero") * final_down.shape[1], final_down.shape[1], axis=1
    )
    part_router = (router_weight * router_gain[:, None]).astype(jnp.bfloat16)
    row_router = gather_directly(part_router, "zero", 0)
    serve_router = lax.all_gather(row_router, "bank", axis=1, tiled=True)
    return (final_gate, final_up, final_down, scale_gate, scale_up, scale_down, serve_router)


def solution(mesh):
    placed = (
        P("bank", "zero", None),
        P("bank", "zero", None),
        P("bank", None, "zero"),
        P("zero", "bank"),
        P("zero"),
    )
    return jax.shard_map(
        local,
        mesh=mesh,
        in_specs=placed,
        out_specs=(
            P("bank", None, "zero"),
            P("bank", None, "zero"),
            P("bank", "zero", None),
            P("bank", "zero"),
            P("bank", "zero"),
            P("bank", "zero"),
            P(),
        ),
        check_vma=False,
    )
```

profile of v0, /device:TPU:224, one launch (start us, length us, event | category | flops | bytes accessed | tf_op | source)
XLA Modules:
  0.0 125.6 jit_solution(8950060846199024515)
XLA Ops:
  0.6 2.2 %abs_reduce_fusion.2 = f32[4,1408]{1,0:T(4,128)S(1)} fusion(f32[4,128,1408]{2,1,0:T(8,128)} %param.5), kind=kLoop, calls=%fused_computation.4 | loop fusion | flops 1436160 | bytes 2906112 | tf_op jit(solution)/shard_map/reduce_sum | solution.py:54
  2.9 0.4 copy-done.1
  3.3 0.2 abs_reduce_fusion.1
  3.6 2.8 %abs_reduce_fusion = f32[4,1408]{1,0:T(4,128)S(1)} fusion(f32[4,1408,128]{2,1,0:T(8,128)} %param.7), kind=kLoop, calls=%fused_computation.2 | loop fusion | flops 1436160 | bytes 2906112 | tf_op jit(solution)/shard_map/reduce_sum | solution.py:56
  6.4 1.5 %broadcast_in_dim.4 = f32[16,1,16896]{2,1,0:T(1,128)} broadcast(f32[16896]{0:T(1024)S(1)} %pad_maximum_fusion.1), dimensions={2} | broadcast | bytes 1148928 | tf_op jit(solution)/shard_map/broadcast_in_dim | solution.py:11
  8.0 7.1 %all-to-all-start = ((f32[16,1,16896]{2,1,0:T(1,128)}), f32[16,1,16896]{2,1,0:T(1,128)}, u32[]{:S(2)}, u32[]{:S(2)}) async-start(f32[16,1,16896]{2,1,0:T(1,128)} %broadcast_in_dim.4), calls=%async_computation | async-start | bytes 2162688 | tf_op jit(solution)/shard_map/all_to_all | solution.py:11
  15.1 2.9 %copy.44 = f32[4,128,1408]{1,0,2:T(4,128)} copy(f32[4,128,1408]{2,1,0:T(8,128)S(1)} %copy-done) | data formatting | bytes 5767168 | tf_op args[0]
  17.9 4.6 %copy.46 = f32[4,128,1408]{1,0,2:T(4,128)} copy(f32[4,128,1408]{2,1,0:T(8,128)} %param.6) | data formatting | bytes 5767168 | tf_op args[1]
  22.6 10.6 %all-to-all-done = f32[16,1,16896]{2,1,0:T(1,128)} async-done(((f32[16,1,16896]{2,1,0:T(1,128)}), f32[16,1,16896]{2,1,0:T(1,128)}, u32[]{:S(2)}, u32[]{:S(2)}) %all-to-all-start) | async-done | bytes 1081376 | tf_op jit(solution)/shard_map/all_to_all | solution.py:11
  33.2 0.6 broadcast_in_dim.5
  33.8 3.5 %all-to-all-start.3 = ((bf16[16,128,4]{1,2,0:T(4,128)(2,1)}), bf16[16,128,4]{1,2,0:T(4,128)(2,1)S(1)}, u32[]{:S(2)}, u32[]{:S(2)}) async-start(bf16[16,128,4]{1,2,0:T(4,128)(2,1)} %broadcast_in_dim.5), calls=%async_computation.3 | async-start | bytes 32768 | tf_op jit(solution)/shard_map/all_to_all | solution.py:11
  37.3 1.9 %reduce_sum.39 = f32[16896]{0:T(1024)S(1)} reduce(f32[16,1,16896]{2,1,0:T(1,128)} %all-to-all-done, f32[]{:T(128)} %constant.6.clone.1), dimensions={0,1}, to_apply=%region_3.0 | reduce | flops 253440 | bytes 1148932 | tf_op jit(solution)/shard_map/reduce_sum | solution.py:15
  39.2 1.2 copy.50
  40.4 7.7 %fusion = bf16[4,1408,128]{2,0,1:T(4,128)(2,1)} fusion(f32[4,1408,128]{2,1,0:T(8,128)S(1)} %copy-done.2, f32[4,1408]{0,1:T(8,128)} %copy.50), kind=kLoop, calls=%fused_computation.5 | loop fusion | flops 1441792 | bytes 4347904 | tf_op jit(solution)/shard_map/convert_element_type | solution.py:66
  48.1 1.2 copy.43
  49.3 1.2 copy.45
  50.5 7.2 %all-to-all-start.2 = ((bf16[4,1408,128]{2,0,1:T(4,128)(2,1)}), bf16[4,1408,128]{2,0,1:T(4,128)(2,1)}, u32[]{:S(2)}, u32[]{:S(2)}) async-start(bf16[4,1408,128]{2,0,1:T(4,128)(2,1)} %fusion), calls=%async_computation.2 | async-start | bytes 2883584 | tf_op jit(solution)/shard_map/all_to_all | solution.py:69
  57.7 6.6 %divide_convert_fusion = (bf16[4,128,1408]{1,0,2:T(4,128)(2,1)S(1)}, bf16[4,128,1408]{1,0,2:T(4,128)(2,1)S(1)}) fusion(f32[4,128,1408]{1,0,2:T(4,128)} %copy.46, f32[4,1408]{0,1:T(8,128)} %copy.45, f32[4,128,1408]{1,0,2:T(4,128)S(1)} %copy-done.3, f32[4,1408]{0,1:T(8,128)} %copy.43), kind=kLoop, calls=%fused_computation.6 | loop fusion | flops 2883584 | bytes 8695808 | tf_op jit(solution)/shard_map/convert_element_type | solution.py:65
  64.2 2.6 %pad_maximum_fusion = bf16[8,128,1408]{1,0,2:T(8,128)(2,1)} fusion(bf16[4,128,1408]{1,0,2:T(4,128)(2,1)S(1)} %get-tuple-element.12, bf16[4,128,1408]{1,0,2:T(4,128)(2,1)S(1)} %get-tuple-element.13), kind=kLoop, calls=%fused_computation | loop fusion | flops 5767168 | bytes 5767168 | tf_op jit(solution)/shard_map/concatenate | solution.py:28
  66.9 12.0 %all-to-all-done.2 = bf16[4,1408,128]{2,0,1:T(4,128)(2,1)} async-done(((bf16[4,1408,128]{2,0,1:T(4,128)(2,1)}), bf16[4,1408,128]{2,0,1:T(4,128)(2,1)}, u32[]{:S(2)}, u32[]{:S(2)}) %all-to-all-start.2) | async-done | bytes 1441824 | tf_op jit(solution)/shard_map/all_to_all | solution.py:69
  78.8 3.7 %all-to-all-start.1 = ((bf16[8,128,1408]{1,0,2:T(8,128)(2,1)}), bf16[8,128,1408]{1,0,2:T(8,128)(2,1)S(1)}, u32[]{:S(2)}, u32[]{:S(2)}) async-start(bf16[8,128,1408]{1,0,2:T(8,128)(2,1)} %pad_maximum_fusion), calls=%async_computation.1 | async-start | bytes 5767168 | tf_op jit(solution)/shard_map/all_to_all | solution.py:30
  82.6 14.6 %all-gather = bf16[16,4,2048]{2,1,0:T(4,128)(2,1)S(1)} all-gather(bf16[1,4,2048]{2,1,0:T(4,128)(2,1)S(1)} %bitcast.28), channel_id=1, replica_groups=mesh['bank'=16,'zero'=16] {'bank'}, dimensions={0}, use_global_device_ids=true | all-gather | bytes 278528 | tf_op jit(solution)/shard_map/all_gather | solution.py:81
  97.2 0.8 reshape.77
  98.0 0.6 constant_dynamic-slice_fusion.2
  98.6 0.7 constant_dynamic-slice_fusion
  99.3 3.0 %copy.52 = bf16[4,88,16,128]{3,2,1,0:T(8,128)(2,1)} copy(bf16[4,88,16,128]{3,0,1,2:T(4,128)(2,1)} %bitcast.4) | data formatting | bytes 2883584 | tf_op jit(solution)/shard_map/all_to_all | solution.py:69
  102.3 3.5 %all_to_all.38 = bf16[4,88,2048]{2,1,0:T(8,128)(2,1)} reshape(bf16[4,88,16,128]{3,2,1,0:T(8,128)(2,1)} %copy.52) | data formatting | bytes 2883584 | tf_op jit(solution)/shard_map/all_to_all | solution.py:69
  105.8 16.3 %all-to-all-done.1 = bf16[8,128,1408]{1,0,2:T(8,128)(2,1)S(1)} async-done(((bf16[8,128,1408]{1,0,2:T(8,128)(2,1)}), bf16[8,128,1408]{1,0,2:T(8,128)(2,1)S(1)}, u32[]{:S(2)}, u32[]{:S(2)}) %all-to-all-start.1) | async-done | bytes 2883616 | tf_op jit(solution)/shard_map/all_to_all | solution.py:30
  122.0 0.4 copy.47
  122.4 0.2 slice_bitcast_fusion
  122.6 1.5 %copy.64 = bf16[4,16,11,8,128]{4,3,1,2,0:T(8,128)(2,1)} copy(bf16[4,16,11,8,128]{4,3,2,1,0:T(8,128)(2,1)S(1)} %get-tuple-element.7) | data formatting | bytes 2883584 | tf_op jit(solution)/shard_map/slice | solution.py:35
  124.1 1.5 %copy.65 = bf16[4,16,11,8,128]{4,3,1,2,0:T(8,128)(2,1)} copy(bf16[4,16,11,8,128]{4,3,2,1,0:T(8,128)(2,1)S(1)} %get-tuple-element.8) | data formatting | bytes 2883584 | tf_op jit(solution)/shard_map/slice | solution.py:35
  (21 shorter events, 0.1 us)
Async XLA Ops:
  0.6 2.7 %copy-start.1 = (f32[4,128,1408]{2,1,0:T(8,128)S(1)}, f32[4,128,1408]{2,1,0:T(8,128)}, u32[]{:S(2)}) copy-start(f32[4,128,1408]{2,1,0:T(8,128)} %param.6) | copy-start | bytes 8650756
  3.6 11.5 %copy-start = (f32[4,128,1408]{2,1,0:T(8,128)S(1)}, f32[4,128,1408]{2,1,0:T(8,128)}, u32[]{:S(2)}) copy-start(f32[4,128,1408]{2,1,0:T(8,128)} %param.5) | copy-start | bytes 8650756
  8.0 25.2 %all-to-all-start = ((f32[16,1,16896]{2,1,0:T(1,128)}), f32[16,1,16896]{2,1,0:T(1,128)}, u32[]{:S(2)}, u32[]{:S(2)}) async-start(f32[16,1,16896]{2,1,0:T(1,128)} %broadcast_in_dim.4), calls=%async_computation | async-start | bytes 2162688 | tf_op jit(solution)/shard_map/all_to_all | solution.py:11
  17.9 4.7 %copy-start.4 = (f32[128,4]{0,1:T(4,128)S(1)}, f32[128,4]{0,1:T(4,128)}, u32[]{:S(2)}) copy-start(f32[128,4]{0,1:T(4,128)} %param.8) | copy-start | bytes 6148
  17.9 4.7 %copy-start.5 = (f32[128]{0:T(128)S(1)}, f32[128]{0:T(128)}, u32[]{:S(2)}) copy-start(f32[128]{0:T(128)} %param.9) | copy-start | bytes 1540
  17.9 22.5 %copy-start.2 = (f32[4,1408,128]{2,1,0:T(8,128)S(1)}, f32[4,1408,128]{2,1,0:T(8,128)}, u32[]{:S(2)}) copy-start(f32[4,1408,128]{2,1,0:T(8,128)} %param.7) | copy-start | bytes 8650756
  33.8 16.7 %all-to-all-start.3 = ((bf16[16,128,4]{1,2,0:T(4,128)(2,1)}), bf16[16,128,4]{1,2,0:T(4,128)(2,1)S(1)}, u32[]{:S(2)}, u32[]{:S(2)}) async-start(bf16[16,128,4]{1,2,0:T(4,128)(2,1)} %broadcast_in_dim.5), calls=%async_computation.3 | async-start | bytes 32768 | tf_op jit(solution)/shard_map/all_to_all | solution.py:11
  48.1 9.6 %copy-start.3 = (f32[4,128,1408]{1,0,2:T(4,128)S(1)}, f32[4,128,1408]{1,0,2:T(4,128)}, u32[]{:S(2)}) copy-start(f32[4,128,1408]{1,0,2:T(4,128)} %copy.44) | copy-start | bytes 8650756
  50.5 28.4 %all-to-all-start.2 = ((bf16[4,1408,128]{2,0,1:T(4,128)(2,1)}), bf16[4,1408,128]{2,0,1:T(4,128)(2,1)}, u32[]{:S(2)}, u32[]{:S(2)}) async-start(bf16[4,1408,128]{2,0,1:T(4,128)(2,1)} %fusion), calls=%async_computation.2 | async-start | bytes 2883584 | tf_op jit(solution)/shard_map/all_to_all | solution.py:69
  78.8 43.2 %all-to-all-start.1 = ((bf16[8,128,1408]{1,0,2:T(8,128)(2,1)}), bf16[8,128,1408]{1,0,2:T(8,128)(2,1)S(1)}, u32[]{:S(2)}, u32[]{:S(2)}) async-start(bf16[8,128,1408]{1,0,2:T(8,128)(2,1)} %pad_maximum_fusion), calls=%async_computation.1 | async-start | bytes 5767168 | tf_op jit(solution)/shard_map/all_to_all | solution.py:30
where the time goes:
time: 126 us
  waiting for transfers between devices  38.8 us (31%)
  local copies, waits for them, and re-layouts  25.8 us (20%)
  other arithmetic  24.1 us (19%)
  starting transfers between devices  21.5 us (17%)
  blocking collectives  14.6 us (12%)
    all_to_all x1, waiting for transfers between devices, side_by_side(): lax.all_to_all(both, axis, split_axis=split_dim, concat_axis=concat_dim,...  16.3 us
    all_gather x1, blocking collectives, local(): serve_router = lax.all_gather(row_router, 'bank', axis=1, tiled=True)  14.6 us
    all_to_all x1, waiting for transfers between devices, local(): lax.all_to_all(narrow_down, 'zero', split_axis=1, concat_axis=2, tiled=True)  12 us
    all_to_all x2, waiting for transfers between devices, copy_for_each(): lax.all_to_all(jnp.broadcast_to(x[None], (count, *x.shape)), axis, 0, 0,...  10.6 us
    all_to_all x2, starting transfers between devices, copy_for_each(): lax.all_to_all(jnp.broadcast_to(x[None], (count, *x.shape)), axis, 0, 0,...  10.6 us
    unnamed x16, local copies, waits for them, and re-layouts  8.94 us
    convert_element_type x1, other arithmetic, local(): (master_down / jnp.expand_dims(scale_down, 2)).astype(jnp.bfloat16)  7.73 us
    all_to_all x1, starting transfers between devices, local(): lax.all_to_all(narrow_down, 'zero', split_axis=1, concat_axis=2, tiled=True)  7.2 us
  transfers between devices with their start and end apart: 4, of which 3 were waited for; matrix products, arithmetic and copies ran while one was open for 28% of the time, Pallas kernels for 0%

commit v1 on v0

--- a/solution.py
+++ b/solution.py
@@ -78,7 +78,8 @@
     )
     part_router = (router_weight * router_gain[:, None]).astype(jnp.bfloat16)
     row_router = gather_directly(part_router, "zero", 0)
-    serve_router = lax.all_gather(row_router, "bank", axis=1, tiled=True)
+    sent = jnp.stack([row_router] * lax.axis_size("bank"))
+    serve_router = jnp.concatenate(lax.all_to_all(sent, "bank", 0, 0), axis=1)
     return (final_gate, final_up, final_down, scale_gate, scale_up, scale_down, serve_router)
 
 

time: 126 us -> 145 us (1.15)
  the two profiles are of different devices: /device:TPU:224 before, /device:TPU:1 now
where the time goes in v1:
time: 145 us; the launch traced here: 144 us
  waiting for transfers between devices  59.3 us (41%)
  starting transfers between devices  33 us (23%)
  local copies, waits for them, and re-layouts  26 us (18%)
  other arithmetic  24.8 us (17%)
    all_to_all x1, waiting for transfers between devices, side_by_side(): lax.all_to_all(both, axis, split_axis=split_dim, concat_axis=concat_dim,...  34.2 us
    all_to_all x1, waiting for transfers between devices, local(): lax.all_to_all(narrow_down, 'zero', split_axis=1, concat_axis=2, tiled=True)  15.3 us
    all_to_all x2, starting transfers between devices, copy_for_each(): lax.all_to_all(jnp.broadcast_to(x[None], (count, *x.shape)), axis, 0, 0,...  13 us
    all_to_all x1, starting transfers between devices, local(): serve_router = jnp.concatenate(lax.all_to_all(sent, 'bank', 0, 0), axis=1)  11.5 us
    all_to_all x2, waiting for transfers between devices, copy_for_each(): lax.all_to_all(jnp.broadcast_to(x[None], (count, *x.shape)), axis, 0, 0,...  9.77 us
    convert_element_type x1, other arithmetic, local(): (master_down / jnp.expand_dims(scale_down, 2)).astype(jnp.bfloat16)  7.73 us
    unnamed x11, local copies, waits for them, and re-layouts  7.58 us
    convert_element_type x1, other arithmetic, local(): (master_up / jnp.expand_dims(scale_up, 1)).astype(jnp.bfloat16)  6.56 us
  transfers between devices with their start and end apart: 5, of which 4 were waited for; matrix products, arithmetic and copies ran while one was open for 28% of the time, Pallas kernels for 0%

profile of v1, /device:TPU:1, one launch (start us, length us, event | category | flops | bytes accessed | tf_op | source)
XLA Modules:
  0.0 143.9 jit_solution(17413675191629362174)
XLA Ops:
  0.6 0.8 multiply_convert_fusion
  1.5 0.6 broadcast_in_dim.5
  2.1 7.6 %all-to-all-start.3 = ((bf16[16,128,4]{1,2,0:T(4,128)(2,1)}), bf16[16,128,4]{1,2,0:T(4,128)(2,1)S(1)}, u32[]{:S(2)}, u32[]{:S(2)}) async-start(bf16[16,128,4]{1,2,0:T(4,128)(2,1)} %broadcast_in_dim.5), calls=%async_computation.3 | async-start | bytes 32768 | tf_op jit(solution)/shard_map/all_to_all | solution.py:11
  9.7 2.1 %abs_reduce_fusion.2 = f32[4,1408]{1,0:T(4,128)S(1)} fusion(f32[4,128,1408]{2,1,0:T(8,128)} %param.5), kind=kLoop, calls=%fused_computation.4 | loop fusion | flops 1436160 | bytes 2906112 | tf_op jit(solution)/shard_map/reduce_sum | solution.py:54
  12.1 2.8 %abs_reduce_fusion = f32[4,1408]{1,0:T(4,128)S(1)} fusion(f32[4,1408,128]{2,1,0:T(8,128)} %param.7), kind=kLoop, calls=%fused_computation.2 | loop fusion | flops 1436160 | bytes 2906112 | tf_op jit(solution)/shard_map/reduce_sum | solution.py:56
  14.9 1.2 all-to-all-done.3
  16.1 1.5 %broadcast_in_dim.4 = f32[16,1,16896]{2,1,0:T(1,128)} broadcast(f32[16896]{0:T(1024)S(1)} %pad_maximum_fusion.1), dimensions={2} | broadcast | bytes 1148928 | tf_op jit(solution)/shard_map/broadcast_in_dim | solution.py:11
  17.7 5.5 %all-to-all-start = ((f32[16,1,16896]{2,1,0:T(1,128)}), f32[16,1,16896]{2,1,0:T(1,128)}, u32[]{:S(2)}, u32[]{:S(2)}) async-start(f32[16,1,16896]{2,1,0:T(1,128)} %broadcast_in_dim.4), calls=%async_computation | async-start | bytes 2162688 | tf_op jit(solution)/shard_map/all_to_all | solution.py:11
  23.1 2.9 %copy.44 = f32[4,128,1408]{1,0,2:T(4,128)} copy(f32[4,128,1408]{2,1,0:T(8,128)S(1)} %copy-done) | data formatting | bytes 5767168 | tf_op args[0]
  26.0 4.5 %copy.46 = f32[4,128,1408]{1,0,2:T(4,128)} copy(f32[4,128,1408]{2,1,0:T(8,128)} %param.6) | data formatting | bytes 5767168 | tf_op args[1]
  30.5 8.5 %all-to-all-done = f32[16,1,16896]{2,1,0:T(1,128)} async-done(((f32[16,1,16896]{2,1,0:T(1,128)}), f32[16,1,16896]{2,1,0:T(1,128)}, u32[]{:S(2)}, u32[]{:S(2)}) %all-to-all-start) | async-done | bytes 1081376 | tf_op jit(solution)/shard_map/all_to_all | solution.py:11
  39.0 0.8 stack.3
  39.8 11.5 %all-to-all-start.4 = ((bf16[16,2048,4]{1,2,0:T(4,128)(2,1)}), bf16[16,2048,4]{1,2,0:T(4,128)(2,1)S(1)}, u32[]{:S(2)}, u32[]{:S(2)}) async-start(bf16[16,2048,4]{1,2,0:T(4,128)(2,1)} %stack.3), calls=%async_computation.4 | async-start | bytes 524288 | tf_op jit(solution)/shard_map/all_to_all | solution.py:82
  51.4 1.9 %reduce_sum.39 = f32[16896]{0:T(1024)S(1)} reduce(f32[16,1,16896]{2,1,0:T(1,128)} %all-to-all-done, f32[]{:T(128)} %constant.6.clone.1), dimensions={0,1}, to_apply=%region_3.0 | reduce | flops 253440 | bytes 1148932 | tf_op jit(solution)/shard_map/reduce_sum | solution.py:15
  53.3 1.2 copy.43
  54.5 1.2 copy.45
  55.7 1.2 copy.50
  56.8 7.7 %fusion = bf16[4,1408,128]{2,0,1:T(4,128)(2,1)} fusion(f32[4,1408,128]{2,1,0:T(8,128)S(1)} %copy-done.2, f32[4,1408]{0,1:T(8,128)} %copy.50), kind=kLoop, calls=%fused_computation.5 | loop fusion | flops 1441792 | bytes 4347904 | tf_op jit(solution)/shard_map/convert_element_type | solution.py:66
  64.6 4.7 %all-to-all-start.2 = ((bf16[4,1408,128]{2,0,1:T(4,128)(2,1)}), bf16[4,1408,128]{2,0,1:T(4,128)(2,1)}, u32[]{:S(2)}, u32[]{:S(2)}) async-start(bf16[4,1408,128]{2,0,1:T(4,128)(2,1)} %fusion), calls=%async_computation.2 | async-start | bytes 2883584 | tf_op jit(solution)/shard_map/all_to_all | solution.py:69
  69.3 6.6 %divide_convert_fusion = (bf16[4,128,1408]{1,0,2:T(4,128)(2,1)S(1)}, bf16[4,128,1408]{1,0,2:T(4,128)(2,1)S(1)}) fusion(f32[4,128,1408]{1,0,2:T(4,128)} %copy.46, f32[4,1408]{0,1:T(8,128)} %copy.45, f32[4,128,1408]{1,0,2:T(4,128)S(1)} %copy-done.3, f32[4,1408]{0,1:T(8,128)} %copy.43), kind=kLoop, calls=%fused_computation.6 | loop fusion | flops 2883584 | bytes 8695808 | tf_op jit(solution)/shard_map/convert_element_type | solution.py:65
  75.8 2.6 %pad_maximum_fusion = bf16[8,128,1408]{1,0,2:T(8,128)(2,1)} fusion(bf16[4,128,1408]{1,0,2:T(4,128)(2,1)S(1)} %get-tuple-element.12, bf16[4,128,1408]{1,0,2:T(4,128)(2,1)S(1)} %get-tuple-element.13), kind=kLoop, calls=%fused_computation | loop fusion | flops 5767168 | bytes 5767168 | tf_op jit(solution)/shard_map/concatenate | solution.py:28
  78.5 15.3 %all-to-all-done.2 = bf16[4,1408,128]{2,0,1:T(4,128)(2,1)} async-done(((bf16[4,1408,128]{2,0,1:T(4,128)(2,1)}), bf16[4,1408,128]{2,0,1:T(4,128)(2,1)}, u32[]{:S(2)}, u32[]{:S(2)}) %all-to-all-start.2) | async-done | bytes 1441824 | tf_op jit(solution)/shard_map/all_to_all | solution.py:69
  93.8 3.7 %all-to-all-start.1 = ((bf16[8,128,1408]{1,0,2:T(8,128)(2,1)}), bf16[8,128,1408]{1,0,2:T(8,128)(2,1)S(1)}, u32[]{:S(2)}, u32[]{:S(2)}) async-start(bf16[8,128,1408]{1,0,2:T(8,128)(2,1)} %pad_maximum_fusion), calls=%async_computation.1 | async-start | bytes 5767168 | tf_op jit(solution)/shard_map/all_to_all | solution.py:30
  97.5 0.8 reshape.81
  98.3 0.6 constant_dynamic-slice_fusion.2
  98.9 0.7 constant_dynamic-slice_fusion
  99.6 3.0 %copy.52 = bf16[4,88,16,128]{3,2,1,0:T(8,128)(2,1)} copy(bf16[4,88,16,128]{3,0,1,2:T(4,128)(2,1)} %bitcast.4) | data formatting | bytes 2883584 | tf_op jit(solution)/shard_map/all_to_all | solution.py:69
  102.6 3.5 %all_to_all.41 = bf16[4,88,2048]{2,1,0:T(8,128)(2,1)} reshape(bf16[4,88,16,128]{3,2,1,0:T(8,128)(2,1)} %copy.52) | data formatting | bytes 2883584 | tf_op jit(solution)/shard_map/all_to_all | solution.py:69
  106.1 34.2 %all-to-all-done.1 = bf16[8,128,1408]{1,0,2:T(8,128)(2,1)S(1)} async-done(((bf16[8,128,1408]{1,0,2:T(8,128)(2,1)}), bf16[8,128,1408]{1,0,2:T(8,128)(2,1)S(1)}, u32[]{:S(2)}, u32[]{:S(2)}) %all-to-all-start.1) | async-done | bytes 2883616 | tf_op jit(solution)/shard_map/all_to_all | solution.py:30
  140.3 0.4 copy.47
  140.9 1.5 %copy.64 = bf16[4,16,11,8,128]{4,3,1,2,0:T(8,128)(2,1)} copy(bf16[4,16,11,8,128]{4,3,2,1,0:T(8,128)(2,1)S(1)} %get-tuple-element.7) | data formatting | bytes 2883584 | tf_op jit(solution)/shard_map/slice | solution.py:35
  142.4 1.5 %copy.65 = bf16[4,16,11,8,128]{4,3,1,2,0:T(8,128)(2,1)} copy(bf16[4,16,11,8,128]{4,3,2,1,0:T(8,128)(2,1)S(1)} %get-tuple-element.8) | data formatting | bytes 2883584 | tf_op jit(solution)/shard_map/slice | solution.py:35
  (19 shorter events, 0.6 us)
Async XLA Ops:
  0.6 11.1 %copy-start.1 = (f32[4,128,1408]{2,1,0:T(8,128)S(1)}, f32[4,128,1408]{2,1,0:T(8,128)}, u32[]{:S(2)}) copy-start(f32[4,128,1408]{2,1,0:T(8,128)} %param.6) | copy-start | bytes 8650756
  2.1 14.0 %all-to-all-start.3 = ((bf16[16,128,4]{1,2,0:T(4,128)(2,1)}), bf16[16,128,4]{1,2,0:T(4,128)(2,1)S(1)}, u32[]{:S(2)}, u32[]{:S(2)}) async-start(bf16[16,128,4]{1,2,0:T(4,128)(2,1)} %broadcast_in_dim.5), calls=%async_computation.3 | async-start | bytes 32768 | tf_op jit(solution)/shard_map/all_to_all | solution.py:11
  12.0 11.1 %copy-start = (f32[4,128,1408]{2,1,0:T(8,128)S(1)}, f32[4,128,1408]{2,1,0:T(8,128)}, u32[]{:S(2)}) copy-start(f32[4,128,1408]{2,1,0:T(8,128)} %param.5) | copy-start | bytes 8650756
  17.7 21.4 %all-to-all-start = ((f32[16,1,16896]{2,1,0:T(1,128)}), f32[16,1,16896]{2,1,0:T(1,128)}, u32[]{:S(2)}, u32[]{:S(2)}) async-start(f32[16,1,16896]{2,1,0:T(1,128)} %broadcast_in_dim.4), calls=%async_computation | async-start | bytes 2162688 | tf_op jit(solution)/shard_map/all_to_all | solution.py:11
  30.5 26.4 %copy-start.2 = (f32[4,1408,128]{2,1,0:T(8,128)S(1)}, f32[4,1408,128]{2,1,0:T(8,128)}, u32[]{:S(2)}) copy-start(f32[4,1408,128]{2,1,0:T(8,128)} %param.7) | copy-start | bytes 8650756
  39.8 24.7 %all-to-all-start.4 = ((bf16[16,2048,4]{1,2,0:T(4,128)(2,1)}), bf16[16,2048,4]{1,2,0:T(4,128)(2,1)S(1)}, u32[]{:S(2)}, u32[]{:S(2)}) async-start(bf16[16,2048,4]{1,2,0:T(4,128)(2,1)} %stack.3), calls=%async_computation.4 | async-start | bytes 524288 | tf_op jit(solution)/shard_map/all_to_all | solution.py:82
  64.6 4.7 %copy-start.3 = (f32[4,128,1408]{1,0,2:T(4,128)S(1)}, f32[4,128,1408]{1,0,2:T(4,128)}, u32[]{:S(2)}) copy-start(f32[4,128,1408]{1,0,2:T(4,128)} %copy.44) | copy-start | bytes 8650756
  64.6 29.2 %all-to-all-start.2 = ((bf16[4,1408,128]{2,0,1:T(4,128)(2,1)}), bf16[4,1408,128]{2,0,1:T(4,128)(2,1)}, u32[]{:S(2)}, u32[]{:S(2)}) async-start(bf16[4,1408,128]{2,0,1:T(4,128)(2,1)} %fusion), calls=%async_computation.2 | async-start | bytes 2883584 | tf_op jit(solution)/shard_map/all_to_all | solution.py:69
  93.8 46.5 %all-to-all-start.1 = ((bf16[8,128,1408]{1,0,2:T(8,128)(2,1)}), bf16[8,128,1408]{1,0,2:T(8,128)(2,1)S(1)}, u32[]{:S(2)}, u32[]{:S(2)}) async-start(bf16[8,128,1408]{1,0,2:T(8,128)(2,1)} %pad_maximum_fusion), calls=%async_computation.1 | async-start | bytes 5767168 | tf_op jit(solution)/shard_map/all_to_all | solution.py:30
